TPU v7x, 32 devices: a whole 2x2x4 slice. The times are simulated.
32 devices in a mesh: samp: 8 (over z, y), snp: 4 (over x, core).
Axes of the slice: x: 2, y: 2, z: 4, core: 2. Of those that a mesh axis runs over, the one named last changes fastest.
Arguments:
- geno_words: int32 [2048, 1024], P('samp', 'snp'), may hold values from -2147483648 to 2147483647, as said below
- counts: int32 [2048], P('samp'), may hold values from 0 to 4, as said below
- probes: bfloat16 [2048, 64], P('samp'), may hold values from -6 to 6
- phenotype: float32 [2048], P('samp'), may hold values from -6 to 6
- tile_comp: int32 [128], replicated, may hold values from 0 to 7, as said below
Outputs:
- images: bfloat16 [2048, 512], P(('samp', 'snp'))
- traces: float32 [8, 8], replicated
- yky: float32 [8], replicated
Inputs may be any that keep to these rules, and one draw needn't show every extreme that they name: `geno_words`: each word packs sixteen dosages of one sample in 2-bit fields as step one reads them; every field holds 0, 1 or 2. `counts`: at least one sample has a count of one or more. `tile_comp`: every component owns at least one tile.
All inputs are finite; a program needn't handle non-finite values.
Results may differ from a plain program's by a relative error of at most 0.015.
Values may be sent and summed in bfloat16 or wider, within the bound.
A program may use at most 64 MiB of HBM per device.

v0:
```python
import jax
import jax.numpy as jnp
from jax import lax
from jax.sharding import PartitionSpec as P

SNPS = 16384
COMPS = 8
EPSILON = 1e-05


def unpack_rows(packed):
    height = packed.shape[0]
    grouped = packed.reshape(height, -1, 1, 128)
    shifts = 2 * jnp.arange(16, dtype=jnp.int32).reshape(1, 1, 16, 1)
    fields = jnp.right_shift(grouped, shifts) & 3
    return fields.reshape(height, -1).astype(jnp.bfloat16)


def block_number(row_count):
    number = 1
    while row_count // number > 768 or row_count % number != 0:
        number = number + 1
    return number


def finish(panel_part, moment_part, totals, inverse, member):
    weight_total = totals[0]
    pheno_total = totals[1]
    probe_total = totals[2:]
    average = moment_part[0] / weight_total
    second = moment_part[1] / weight_total
    spread = 1.0 / jnp.sqrt(second - average * average + EPSILON)
    unit_panel = spread[:, None] * (panel_part - average[:, None] * probe_total[None, :])
    pheno_unit = spread * (moment_part[2] - average * pheno_total)
    coefficients = (spread[:, None] * unit_panel * inverse[:, None]).astype(jnp.bfloat16)
    energy = jnp.sum(member * (pheno_unit * pheno_unit * inverse)[:, None], axis=0)
    return (average, coefficients, energy)


def on_device(geno_words, counts, probes, phenotype, tile_comp):
    height = geno_words.shape[0]
    snp_local = geno_words.shape[1] * 16
    tile_local = snp_local // 128
    probe_count = probes.shape[1]
    weights = counts.astype(jnp.float32)
    root_weight = jnp.sqrt(weights)
    probe_rows = (probes.astype(jnp.float32) * root_weight[:, None]).astype(jnp.bfloat16)
    pheno_rows = (phenotype * root_weight).astype(jnp.bfloat16)
    count_rows = counts.astype(jnp.bfloat16)
    left_rows = jnp.stack([count_rows, pheno_rows], axis=1)
    dosage = unpack_rows(geno_words)
    cross_panel = jnp.einsum("rj,rb->jb", dosage, probe_rows, preferred_element_type=jnp.float32)
    linear = jnp.einsum("rc,rj->cj", left_rows, dosage, preferred_element_type=jnp.float32)
    squares = jnp.einsum("r,rj->j", count_rows, dosage * dosage, preferred_element_type=jnp.float32)
    moments = jnp.stack([linear[0], squares, linear[1]])
    totals = jnp.concatenate(
        [
            jnp.sum(weights)[None],
            jnp.sum(pheno_rows.astype(jnp.float32))[None],
            jnp.sum(probe_rows.astype(jnp.float32), axis=0),
        ]
    )
    levels = jnp.arange(COMPS, dtype=jnp.int32)
    member_all = (tile_comp[:, None] == levels[None, :]).astype(jnp.float32)
    comp_sizes = 128.0 * jnp.sum(member_all, axis=0)
    member_tiles = lax.dynamic_slice_in_dim(
        member_all, lax.axis_index("snp") * tile_local, tile_local, 0
    )
    member_snps = jnp.repeat(member_tiles, 128, axis=0)
    inverse = jnp.sum(member_snps * (1.0 / comp_sizes)[None, :], axis=1)
    summed_panel, summed_moments, totals = lax.psum(
        (cross_panel.reshape(-1, 128), moments, totals), "samp"
    )
    average, coefficients, energy = finish(
        summed_panel.reshape(snp_local, probe_count), summed_moments, totals, inverse, member_snps
    )
    energy = lax.psum(energy, "snp")
    coef_tiles = coefficients.reshape(tile_local, 128, probe_count)
    centre = jnp.sum(average.reshape(tile_local, 128, 1) * coef_tiles.astype(jnp.float32), axis=1)
    quarter = height // lax.axis_size("snp")
    inner_count = block_number(quarter * lax.axis_size("snp"))
    piece_rows = quarter * lax.axis_size("snp") // inner_count
    dosage = unpack_rows(geno_words)
    dosage = dosage.reshape(piece_rows, tile_local, 128)
    partial_value = (
        jnp.einsum("rtj,tjb->rtb", dosage, coef_tiles, preferred_element_type=jnp.float32)
        - centre[None]
    )
    grouped = jnp.einsum(
        "rtb,tk->rkb", partial_value, member_tiles, precision=lax.Precision.HIGHEST
    )
    scaled = grouped * root_weight[:, None, None]
    pieces = scaled.reshape(piece_rows, COMPS * probe_count)
    own_images = lax.psum_scatter(pieces, "snp", scatter_dimension=0, tiled=True)
    stacked = own_images.reshape(quarter, COMPS, probe_count)
    local_trace = jnp.einsum("rkb,rlb->kl", stacked, stacked, precision=lax.Precision.HIGHEST)
    trace_sum = lax.psum(local_trace, ("samp", "snp"))
    weight_total = totals[0]
    traces = trace_sum * (SNPS / (COMPS * probe_count)) / (weight_total * weight_total)
    return (own_images.astype(jnp.bfloat16), traces, energy / weight_total)


def solution(mesh):
    in_specs = (P("samp", "snp"), P("samp"), P("samp", None), P("samp"), P())
    out_specs = (P(("samp", "snp"), None), P(), P())
    return jax.shard_map(
        on_device, mesh=mesh, in_specs=in_specs, out_specs=out_specs, check_vma=False
    )
```

profile of v0, /device:TPU:0, one launch (start us, length us, event | category | flops | bytes accessed | tf_op | source)
XLA Modules:
  0.0 172.9 jit_solution(4429881836668498962)
XLA Ops:
  7.2 1.1 copy.42
  8.3 1.3 convert_reduce_fusion.2
  9.7 0.7 fusion.1
  10.4 0.7 convolution_bitcast_fusion
  11.2 1.1 copy.55
  12.4 0.1 convert_reduce_fusion
  12.5 0.1 convert_reduce_fusion.1
  12.7 0.6 fusion.7
  13.3 0.7 fusion.18
  14.0 1.4 pad_maximum_fusion.1
  15.4 40.4 %all-reduce = (f32[66]{0:T(128)S(1)}, f32[3,4096]{1,0:T(4,128)S(1)}) all-reduce(f32[66]{0:T(128)S(1)} %pad_maximum_fusion.1, f32[3,4096]{1,0:T(4,128)S(1)} %pad_maximum_fusion), channel_id=1, replica_groups=mesh['samp'=8,'snp'=4] {'samp'}, use_global_device_ids=true, to_apply=%region_4.0 | all-reduce | flops 12354 | bytes 98832 | tf_op jit(solution)/shard_map/psum | solution.py:71
  55.9 0.6 fusion.28
  56.8 2.5 %shift_right_arithmetic.41 = s32[256,2,16,128]{0,3,2,1:T(8,128)} broadcast(s32[256,2,128]{0,2,1:T(8,128)S(1)} %bitcast.41), dimensions={0,1,3} | broadcast | bytes 4456448 | tf_op jit(solution)/shard_map/shift_right_arithmetic | solution.py:15
  59.2 5.6 %copy.36 = s32[256,32,128]{2,0,1:T(8,128)} copy(s32[256,32,128]{0,2,1:T(8,128)} %bitcast.38) | data formatting | bytes 8388608 | tf_op jit(solution)/shard_map/shift_right_arithmetic | solution.py:15
  64.8 0.1 multiply_reduce_fusion.2
  64.9 0.7 fusion.26
  65.6 0.7 multiply_multiply_fusion
  66.3 28.1 %all-reduce.3.cloned.1.call-done = f32[32,128,64]{1,2,0:T(8,128)} async-done(((f32[32,128,64]{1,2,0:T(8,128)}), f32[32,128,64]{1,2,0:T(8,128)}) %all-reduce.3.cloned.1.call-update) | async-done | bytes 1048592 | tf_op jit(solution)/shard_map/psum | solution.py:71
  94.4 1.7 multiply_reduce_fusion
  96.0 3.1 %subtract_bitcast_fusion = f32[256,32,64]{0,2,1:T(8,128)S(1)} fusion(bf16[32,128,64]{1,2,0:T(8,128)(2,1)S(1)} %get-tuple-element.18, s32[256,32,128]{2,0,1:T(8,128)} %copy.36, s32[32]{0:T(128)S(1)} %shift_right_arithmetic.49, f32[32,64]{1,0:T(8,128)S(1)} %get-tuple-element.17), kind=kOutput, calls=%fused_computation.7 | convolution fusion | flops 137887744 | bytes 6824064 | tf_op jit(solution)/shard_map/rtj,tjb->rtb/dot_general | solution.py:86
  99.1 2.0 %fusion.12 = f32[256,8,64]{0,1,2:T(8,128)S(1)} fusion(f32[256,32,64]{0,2,1:T(8,128)S(1)} %subtract_bitcast_fusion, f32[256]{0:T(256)S(1)} %get-tuple-element.29, pred[128,8]{0,1:T(8,128)(4,1)S(1)} %get-tuple-element.32, s32[]{:T(128)S(6)} %select_n.3), kind=kOutput, calls=%fused_computation.14 | convolution fusion | flops 50462720 | bytes 2623492 | tf_op jit(solution)/shard_map/rtb,tk->rkb/dot_general | solution.py:89
  101.1 0.2 copy.38
  101.3 1.0 copy.43
  102.3 0.2 multiply_reduce_fusion.1
  102.5 6.5 %psum.39 = f32[8]{0:T(128)S(1)} all-reduce(f32[8]{0:T(128)S(1)} %multiply_reduce_fusion.1), channel_id=1, replica_groups=mesh['samp'=8,'snp'=4] {'snp'}, use_global_device_ids=true, to_apply=%region_12.0 | all-reduce | flops 8 | bytes 64 | tf_op jit(solution)/shard_map/psum | solution.py:77
  110.3 1.2 broadcast_divide_fusion
  111.5 12.2 %reduce-scatter.4.cloned.1.call-done = f32[64,512]{1,0:T(8,128)} async-done(((f32[256,512]{1,0:T(8,128)}), f32[64,512]{1,0:T(8,128)}) %reduce-scatter.4.cloned.1.call-update) | async-done | bytes 131088
  123.7 1.0 copy.44
  124.7 0.7 convolution_bitcast_fusion.1
  125.5 39.3 %psum.38 = f32[8,8]{1,0:T(8,128)S(1)} all-reduce(f32[8,8]{1,0:T(8,128)S(1)} %convolution_bitcast_fusion.1), channel_id=1, replica_groups=mesh['samp'=8,'snp'=4] {'samp','snp'}, use_global_device_ids=true, to_apply=%region_10.0 | all-reduce | flops 64 | bytes 512 | tf_op jit(solution)/shard_map/psum | solution.py:97
  164.8 0.7 copy.41
  165.5 0.6 multiply_divide_fusion
  (25 shorter events, 0.6 us)
Async XLA Ops:
  7.2 3.3 %copy-start = (bf16[256,64]{0,1:T(8,128)(2,1)S(1)}, bf16[256,64]{0,1:T(8,128)(2,1)}, u32[]{:S(2)}) copy-start(bf16[256,64]{0,1:T(8,128)(2,1)} %param.7) | copy-start | bytes 98308
  7.2 87.2 %all-reduce.3.cloned.1.call-start = ((), (), s32[]{:S(2)}) async-start(), calls=%async_computation.1 | async-start | bytes 2097152 | tf_op jit(solution)/shard_map/psum | solution.py:71
  11.2 1.2 copy-start.1
  11.2 1.3 copy-start.2
  12.3 111.4 %reduce-scatter.4.cloned.1.call-start = ((), (), s32[]{:S(2)}) async-start(), calls=%async_computation.2 | async-start | bytes 655360
Sparse Core Ops, SparseCore 0:
  12.4 81.8 all-reduce.2
  102.4 21.2 reduce-scatter.3
where the time goes:
time: 173 us
  blocking collectives  86.2 us (50%)
  waiting for transfers between devices  40.3 us (23%)
  between operations  15.5 us (9%)
  local copies, waits for them, and re-layouts  14.2 us (8%)
  other arithmetic  8.78 us (5%)
  matrix products  7.85 us (5%)
    psum x1, blocking collectives, on_device(): lax.psum((cross_panel.reshape(-1, 128), moments, totals), 'samp')  40.4 us
    psum x1, blocking collectives, on_device(): trace_sum = lax.psum(local_trace, ('samp', 'snp'))  39.3 us
    psum x1, waiting for transfers between devices, on_device(): lax.psum((cross_panel.reshape(-1, 128), moments, totals), 'samp')  28.1 us
    unnamed x3, waiting for transfers between devices  12.2 us
    shift_right_arithmetic x6, local copies, waits for them, and re-layouts, unpack_rows(): fields = jnp.right_shift(grouped, shifts) & 3  9.3 us
    psum x1, blocking collectives, on_device(): energy = lax.psum(energy, 'snp')  6.51 us
  transfers between devices with their start and end apart: 2, of which 2 were waited for; matrix products, arithmetic and copies ran while one was open for 9% of the time, Pallas kernels for 0%

commit v1 on v0

--- a/solution.py
+++ b/solution.py
@@ -94,7 +94,7 @@
     own_images = lax.psum_scatter(pieces, "snp", scatter_dimension=0, tiled=True)
     stacked = own_images.reshape(quarter, COMPS, probe_count)
     local_trace = jnp.einsum("rkb,rlb->kl", stacked, stacked, precision=lax.Precision.HIGHEST)
-    trace_sum = lax.psum(local_trace, ("samp", "snp"))
+    trace_sum = lax.psum(lax.psum(local_trace, "snp"), "samp")
     weight_total = totals[0]
     traces = trace_sum * (SNPS / (COMPS * probe_count)) / (weight_total * weight_total)
     return (own_images.astype(jnp.bfloat16), traces, energy / weight_total)

time: 173 us -> 163 us (0.942)
  blocking collectives: 86.2 us -> 67.9 us
  waiting for transfers between devices: 40.3 us -> 48 us
    psum x2, blocking collectives: 45.8 us -> 27.4 us  [on_device(): trace_sum = lax.psum(lax.psum(local_trace, 'snp'), 'samp')]
    unnamed x3, waiting for transfers between devices: 12.2 us -> 19.9 us
  transfers between devices with their start and end apart: 2 -> 2, of which waited for: 2 -> 2; matrix products, arithmetic and copies ran while one was open for 9% -> 8% of each run, Pallas kernels for 0% -> 0%
where the time goes in v1:
time: 163 us; the launch traced here: 162 us
  blocking collectives  67.9 us (42%)
  waiting for transfers between devices  48 us (29%)
  between operations  15.5 us (10%)
  local copies, waits for them, and re-layouts  14.2 us (9%)
  other arithmetic  8.77 us (5%)
  matrix products  7.85 us (5%)
    psum x1, blocking collectives, on_device(): lax.psum((cross_panel.reshape(-1, 128), moments, totals), 'samp')  40.4 us
    psum x1, waiting for transfers between devices, on_device(): lax.psum((cross_panel.reshape(-1, 128), moments, totals), 'samp')  28.1 us
    psum x2, blocking collectives, on_device(): trace_sum = lax.psum(lax.psum(local_trace, 'snp'), 'samp')  27.4 us
    unnamed x3, waiting for transfers between devices  19.9 us
    shift_right_arithmetic x6, local copies, waits for them, and re-layouts, unpack_rows(): fields = jnp.right_shift(grouped, shifts) & 3  9.3 us
  transfers between devices with their start and end apart: 2, of which 2 were waited for; matrix products, arithmetic and copies ran while one was open for 8% of the time, Pallas kernels for 0%

profile of v1, /device:TPU:0, one launch (start us, length us, event | category | flops | bytes accessed | tf_op | source)
XLA Modules:
  0.0 162.3 jit_solution(14717312680185877962)
XLA Ops:
  7.2 1.1 copy.42
  8.3 1.3 convert_reduce_fusion.2
  9.7 0.7 fusion.1
  10.4 0.7 convolution_bitcast_fusion
  11.2 1.1 copy.55
  12.4 0.1 convert_reduce_fusion
  12.5 0.1 convert_reduce_fusion.1
  12.7 0.6 fusion.7
  13.3 0.7 fusion.18
  14.0 1.4 pad_maximum_fusion.1
  15.4 40.4 %all-reduce = (f32[66]{0:T(128)S(1)}, f32[3,4096]{1,0:T(4,128)S(1)}) all-reduce(f32[66]{0:T(128)S(1)} %pad_maximum_fusion.1, f32[3,4096]{1,0:T(4,128)S(1)} %pad_maximum_fusion), channel_id=1, replica_groups=mesh['samp'=8,'snp'=4] {'samp'}, use_global_device_ids=true, to_apply=%region_4.0 | all-reduce | flops 12354 | bytes 98832 | tf_op jit(solution)/shard_map/psum | solution.py:71
  55.9 0.6 fusion.28
  56.8 2.5 %shift_right_arithmetic.41 = s32[256,2,16,128]{0,3,2,1:T(8,128)} broadcast(s32[256,2,128]{0,2,1:T(8,128)S(1)} %bitcast.41), dimensions={0,1,3} | broadcast | bytes 4456448 | tf_op jit(solution)/shard_map/shift_right_arithmetic | solution.py:15
  59.2 5.6 %copy.36 = s32[256,32,128]{2,0,1:T(8,128)} copy(s32[256,32,128]{0,2,1:T(8,128)} %bitcast.38) | data formatting | bytes 8388608 | tf_op jit(solution)/shard_map/shift_right_arithmetic | solution.py:15
  64.8 0.1 multiply_reduce_fusion.2
  64.9 0.7 fusion.26
  65.6 0.7 multiply_multiply_fusion
  66.3 28.1 %all-reduce.4.cloned.1.call-done = f32[32,128,64]{1,2,0:T(8,128)} async-done(((f32[32,128,64]{1,2,0:T(8,128)}), f32[32,128,64]{1,2,0:T(8,128)}) %all-reduce.4.cloned.1.call-update) | async-done | bytes 1048592 | tf_op jit(solution)/shard_map/psum | solution.py:71
  94.4 1.7 %multiply_reduce_fusion = (f32[32,64]{1,0:T(8,128)S(1)}, bf16[32,128,64]{1,2,0:T(8,128)(2,1)S(1)}) fusion(f32[32,128]{1,0:T(8,128)S(1)} %bitcast.45, f32[32,128]{1,0:T(8,128)S(1)} %multiply_reduce_fusion.2, f32[32,128,64]{1,2,0:T(8,128)} %all-reduce.4.cloned.1.call-done, f32[64]{0:T(128)S(1)} %slice.30, f32[32,128]{1,0:T(8,128)S(1)} %get-tuple-element.27), kind=kLoop, calls=%fused_computation.17 | loop fusion | flops 2357248 | bytes 1630464 | tf_op jit(solution)/shard_map/reduce_sum | solution.py:79
  96.0 3.1 %subtract_bitcast_fusion = f32[256,32,64]{0,2,1:T(8,128)S(1)} fusion(bf16[32,128,64]{1,2,0:T(8,128)(2,1)S(1)} %get-tuple-element.20, s32[256,32,128]{2,0,1:T(8,128)} %copy.36, s32[32]{0:T(128)S(1)} %shift_right_arithmetic.49, f32[32,64]{1,0:T(8,128)S(1)} %get-tuple-element.19), kind=kOutput, calls=%fused_computation.7 | convolution fusion | flops 137887744 | bytes 6824064 | tf_op jit(solution)/shard_map/rtj,tjb->rtb/dot_general | solution.py:86
  99.1 2.0 %fusion.12 = f32[256,8,64]{0,1,2:T(8,128)S(1)} fusion(f32[256,32,64]{0,2,1:T(8,128)S(1)} %subtract_bitcast_fusion, f32[256]{0:T(256)S(1)} %get-tuple-element.31, pred[128,8]{0,1:T(8,128)(4,1)S(1)} %get-tuple-element.34, s32[]{:T(128)S(6)} %select_n.3), kind=kOutput, calls=%fused_computation.14 | convolution fusion | flops 50462720 | bytes 2623492 | tf_op jit(solution)/shard_map/rtb,tk->rkb/dot_general | solution.py:89
  101.1 0.2 copy.38
  101.3 1.0 copy.43
  103.6 0.2 multiply_reduce_fusion.1
  103.8 19.9 %reduce-scatter.4.cloned.1.call-done = f32[64,512]{1,0:T(8,128)} async-done(((f32[256,512]{1,0:T(8,128)}), f32[64,512]{1,0:T(8,128)}) %reduce-scatter.4.cloned.1.call-update) | async-done | bytes 131088
  123.7 1.0 copy.44
  124.7 0.7 convolution_bitcast_fusion.1
  125.5 5.8 %all-reduce.1 = (f32[8,8]{1,0:T(8,128)S(1)}, f32[8]{0:T(128)S(1)}) all-reduce(f32[8,8]{1,0:T(8,128)S(1)} %convolution_bitcast_fusion.1, f32[8]{0:T(128)S(1)} %multiply_reduce_fusion.1), channel_id=1, replica_groups=mesh['samp'=8,'snp'=4] {'snp'}, use_global_device_ids=true, to_apply=%region_10.0 | all-reduce | flops 72 | bytes 576 | tf_op jit(solution)/shard_map/psum | solution.py:97
  131.3 21.6 %psum.46 = f32[8,8]{1,0:T(8,128)S(1)} all-reduce(f32[8,8]{1,0:T(8,128)S(1)} %get-tuple-element.17), channel_id=1, replica_groups=mesh['samp'=8,'snp'=4] {'samp'}, use_global_device_ids=true, to_apply=%region_11.0 | all-reduce | flops 64 | bytes 512 | tf_op jit(solution)/shard_map/psum | solution.py:97
  152.9 1.2 broadcast_divide_fusion
  154.1 0.7 copy.41
  154.8 0.6 multiply_divide_fusion
  (25 shorter events, 0.6 us)
Async XLA Ops:
  7.2 3.3 %copy-start = (bf16[256,64]{0,1:T(8,128)(2,1)S(1)}, bf16[256,64]{0,1:T(8,128)(2,1)}, u32[]{:S(2)}) copy-start(bf16[256,64]{0,1:T(8,128)(2,1)} %param.7) | copy-start | bytes 98308
  7.2 87.2 %all-reduce.4.cloned.1.call-start = ((), (), s32[]{:S(2)}) async-start(), calls=%async_computation.1 | async-start | bytes 2097152 | tf_op jit(solution)/shard_map/psum | solution.py:71
  11.2 1.2 copy-start.1
  11.2 1.3 copy-start.2
  12.3 111.4 %reduce-scatter.4.cloned.1.call-start = ((), (), s32[]{:S(2)}) async-start(), calls=%async_computation.2 | async-start | bytes 655360
Sparse Core Ops, SparseCore 0:
  12.4 81.8 all-reduce.3
  102.4 21.2 reduce-scatter.3
